TPU v7x, 32 devices: a whole 2x2x4 slice. The times are simulated.
32 devices in a mesh: zon: 8 (over z, y), mer: 4 (over x, core).
Axes of the slice: x: 2, y: 2, z: 4, core: 2. Of those that a mesh axis runs over, the one named last changes fastest.
Arguments:
- sea_level: float32 [512, 4096], P('mer', 'zon'), may hold values from -6 to 6
- forcing: float32 [512, 4096], P('mer', 'zon'), may hold values from -6 to 6
- link_weights: float32 [8, 512, 4096], P(None, 'mer', 'zon'), may hold values from 0.1 to 2
- excess: float32 [512, 4096], P('mer', 'zon'), may hold values from 0.05 to 0.5
- ocean_mask: int32 [512, 4096], P('mer', 'zon'), may hold values 0 or 1
- current: float32 [2, 512, 4096], P(None, 'mer', 'zon'), may hold values from -6 to 6
- intersection_block: int32 [32, 32, 32], P(('zon', 'mer')), may hold values from -1 to 511, as said below
- intersection_cols: int32 [32, 32, 32, 128], P(('zon', 'mer')), may hold values from -1 to 127, as said below
- ice_mass: float32 [32, 32, 32, 128], P(('zon', 'mer')), may hold values from 0.2 to 3
- coriolis: float32 [32, 32, 32, 128], P(('zon', 'mer')), may hold values from -1.5 to 1.5
- ice_start: float32 [2, 32, 32, 32, 128], P(None, ('zon', 'mer')), may hold values from -6 to 6
- wind_stress: float32 [2, 32, 32, 32, 128], P(None, ('zon', 'mer')), may hold values from -6 to 6
Outputs:
- surface: float32 [512, 4096], P('mer', 'zon')
- velocity: float32 [2, 32, 32, 32, 128], P(None, ('zon', 'mer'))
Inputs may be any that keep to these rules, and one draw needn't show every extreme that they name: `intersection_block`: for each owner device and ice device, the live ocean block numbers come first among the 32 slots and empty slots hold -1; in every draw one ice device receives 32 live blocks from every owner device. `intersection_cols`: within a live intersection block the cells named by different rows are distinct; rows of empty slots are all -1.
All inputs are finite; a program needn't handle non-finite values. No bound on the sum of `ocean_mask` on one device may be relied on, other than what follows from the above.
Results may differ from a plain program's by a relative error of at most 0.00002.
Values sent between devices are 32-bit elements; how exact they have to be, the bound alone decides.
A program may use at most 256 MiB of HBM per device.

v0:
```python
import functools

import jax
import jax.numpy as jnp
from jax import lax
from jax.experimental import pallas as pl
from jax.experimental.pallas import tpu as pltpu
from jax.sharding import PartitionSpec as P

SWEEPS = 2
ICE_SWEEPS = 3
ROW_RIM = 8
COL_RIM = 16
LANES = 128

drag_coeff = 1.0
link_coeff = 0.5
VM = pl.BlockSpec(memory_space=pltpu.VMEM)
HBM = pl.BlockSpec(memory_space=pltpu.HBM)
TRAVEL_VMEM = 40 * 1024 * 1024
SWEEP_VMEM = 16 * 1024 * 1024


def cost(flops, nbytes):
    return pl.CostEstimate(flops=flops, bytes_accessed=nbytes, transcendentals=0)


def lane_take(values, index):
    return jnp.take_along_axis(values, index, axis=1, mode="promise_in_bounds")


def split3(values):
    high = values.astype(jnp.bfloat16)
    rest = values - high.astype(jnp.float32)
    middle = rest.astype(jnp.bfloat16)
    low = (rest - middle.astype(jnp.float32)).astype(jnp.bfloat16)
    return high, middle, low


def nn_dot(a, b):
    return lax.dot_general(a, b, (((1,), (0,)), ((), ())), preferred_element_type=jnp.float32)


def block_rows(blocks, tiles, rows):
    safe = jnp.maximum(blocks, 0)
    return jnp.where(blocks >= 0, (safe % tiles) * rows + safe // tiles, -1)


def inverse_rows(cols):
    lane = lax.broadcasted_iota(jnp.int32, (8, LANES), 1)
    sub = lax.broadcasted_iota(jnp.int32, (8, LANES), 0)
    order = (lane + 1).astype(jnp.float32)
    index = (lane % 16) * 8 + sub
    group = lane // 16
    high = jnp.right_shift(cols, 4)
    low = jnp.bitwise_and(cols, 15)
    left = jnp.concatenate([jnp.where(high == h, 1.0, 0.0) for h in range(8)], axis=0)
    right = jnp.concatenate([jnp.where(low == b, order, 0.0) for b in range(16)], axis=0)
    product = lax.dot_general(
        left.astype(jnp.bfloat16),
        right.astype(jnp.bfloat16),
        (((1,), (1,)), ((), ())),
        preferred_element_type=jnp.float32,
    )
    found = jnp.zeros((8, LANES), jnp.float32)
    for h in range(8):
        found = jnp.where(group == h, lane_take(product[h * 8 : (h + 1) * 8], index), found)
    return found.astype(jnp.int32) - 1


def ice_block(mass, coriolis, start, wind, current):
    pairs, width = mass.shape
    lane = lax.broadcasted_iota(jnp.int32, (pairs, width), 1)
    first, last = lane == 0, lane == width - 1

    def beside(values):
        before = jnp.where(first, 0.0, pltpu.roll(values, 1, 1))
        after = jnp.where(last, 0.0, pltpu.roll(values, width - 1, 1))
        return before + after

    diagonal = mass + drag_coeff + 2.0 * link_coeff
    turning = coriolis * mass
    inverse = 1.0 / (diagonal * diagonal + turning * turning)
    diagonal = diagonal * inverse
    turning = turning * inverse
    east, north = start
    base_east = mass * east + wind[0] + drag_coeff * current[0]
    base_north = mass * north + wind[1] + drag_coeff * current[1]
    for _ in range(ICE_SWEEPS):
        right_east = base_east + link_coeff * beside(east)
        right_north = base_north + link_coeff * beside(north)
        east = diagonal * right_east + turning * right_north
        north = diagonal * right_north - turning * right_east
    return east, north


def around(sizes, body_ref, edge_ref, east_ref, west_ref, south_ref, north_ref, send, recv):
    rows = body_ref.shape[1]
    nz, nm = sizes
    z, m = lax.axis_index("zon"), lax.axis_index("mer")
    top, end = pl.ds(0, ROW_RIM), pl.ds(rows - ROW_RIM, ROW_RIM)
    whole, after, before = pl.ds(0, rows), pl.ds(rows, ROW_RIM), pl.ds(rows + ROW_RIM, ROW_RIM)
    moves = [
        (edge_ref.at[0], east_ref.at[whole], -1, 0),
        (edge_ref.at[1], west_ref.at[whole], 1, 0),
        (body_ref.at[:, top], south_ref, 0, -1),
        (body_ref.at[:, end], north_ref, 0, 1),
        (edge_ref.at[0, top], east_ref.at[after], -1, -1),
        (edge_ref.at[0, end], east_ref.at[before], -1, 1),
        (edge_ref.at[1, top], west_ref.at[after], 1, -1),
        (edge_ref.at[1, end], west_ref.at[before], 1, 1),
    ]
    return [
        pltpu.make_async_remote_copy(
            src_ref=source,
            dst_ref=target,
            send_sem=send.at[i],
            recv_sem=recv.at[i],
            device_id={"zon": lax.rem(z + dz + nz, nz), "mer": lax.rem(m + dm + nm, nm)},
            device_id_type=pl.DeviceIdType.MESH,
        )
        for i, (source, target, dz, dm) in enumerate(moves)
    ]


def pick_group(base, per, turned_ids, parts, cols_ref, values_ref, lanes_ref, group):
    pairs = cols_ref.shape[1]
    lane = lax.broadcasted_iota(jnp.int32, (LANES, LANES), 1)
    turned = jnp.concatenate(
        [
            lane_take(turned_ids, jnp.full((pairs, LANES), base + d, jnp.int32))
            for d in range(per)
        ],
        axis=0,
    )
    lanes_ref[group] = jnp.transpose(turned)[:8]
    pick = jnp.concatenate(
        [
            jnp.where(turned == lane + b * LANES, 1.0, 0.0).astype(jnp.bfloat16)
            for b in range(parts.shape[1] // LANES)
        ],
        axis=1,
    )
    picked = nn_dot(pick, parts[0]) + nn_dot(pick, parts[1]) + nn_dot(pick, parts[2])
    cols = cols_ref[pl.ds(base, per)].reshape(LANES, LANES)
    index = jnp.maximum(cols, 0)
    for c in range(2):
        taken = lane_take(picked[:, c * LANES : (c + 1) * LANES], index)
        taken = jnp.where(cols >= 0, taken, 0.0)
        for d in range(per):
            values_ref[base + d, c] = taken[d * pairs : (d + 1) * pairs]


def put_group(base, per, returned_ref, inverse_ref, lanes_ref, group, count):
    pairs = inverse_ref.shape[1]
    row = lax.broadcasted_iota(jnp.int32, (count, LANES), 0)
    ids = lanes_ref[group]
    put = jnp.where(
        jnp.broadcast_to(ids[:1], (count, LANES)) == row, 1.0, 0.0
    ).astype(jnp.bfloat16)
    inverse = inverse_ref[pl.ds(base, per)].reshape(LANES, LANES)
    index = jnp.maximum(inverse, 0)
    halves = []
    for c in range(2):
        values = jnp.concatenate([returned_ref[base + d, c] for d in range(per)], axis=0)
        halves.append(jnp.where(inverse >= 0, lane_take(values, index), 0.0))
    high, middle, low = split3(jnp.concatenate(halves, axis=1))
    return nn_dot(put, high) + nn_dot(put, middle) + nn_dot(put, low)


def side_tile(k, east_ref, west_ref, known):
    tall = east_ref.shape[0]
    per = LANES // COL_RIM
    slot = lax.broadcasted_iota(jnp.int32, (tall, LANES), 1) // COL_RIM
    at = (k // per) * LANES
    spot = k % per
    east = east_ref[:, at : at + LANES]
    west = west_ref[:, at : at + LANES]
    if spot:
        east = pltpu.roll(east, LANES - spot * COL_RIM, 1)
    if spot != per - 1:
        west = pltpu.roll(west, LANES - (spot + 1) * COL_RIM, 1)
    both = jnp.where(slot == 0, east, jnp.where(slot == per - 1, west, 0.0))
    return jnp.where(known, both, 0.0)


def known_rows(sizes, rows, tall):
    m = lax.axis_index("mer")
    row = lax.broadcasted_iota(jnp.int32, (tall, LANES), 0)
    lower = jnp.where(m == sizes[1] - 1, rows, rows + ROW_RIM)
    upper = jnp.where(m == 0, tall, rows + ROW_RIM)
    return (row < lower) | ((row >= rows + ROW_RIM) & (row >= upper))


def travel_kernel(
    sizes,
    current_hbm, blocks_hbm, cols_hbm, mass_hbm, coriolis_hbm, start_hbm, wind_hbm,
    sea_hbm, forcing_hbm, weights_hbm, excess_hbm, mask_hbm,
    velocity_ref, halves_ref, stress_ref, late_east, late_west, late_south, late_north,
    current_ref, blocks_ref, square, cols_ref, mass_ref, coriolis_ref, start_ref, wind_ref,
    sea_ref, forcing_ref, weights_ref, excess_ref, mask_ref,
    parts, lanes_ref, values_ref, arrived, drag, returned_ref, inverse_ref, total,
    body_ref, edge, east_ref, west_ref, south_ref, north_ref, field, stress_edge,
    loads, send_out, recv_out, send_back, recv_back, send_rim, recv_rim, send_late, recv_late,
):
    nz, nm = sizes
    count = nz * nm
    z, m = lax.axis_index("zon"), lax.axis_index("mer")
    me = z * nm + m
    _, rows, width = current_ref.shape
    tiles = width // LANES
    devices, pairs, _ = cols_ref.shape
    per = LANES // pairs
    span = per // nm
    groups = count // per
    mine = lax.div(z, span)

    def group_of(i):
        return lax.rem(mine + groups // 2 + lax.div(i + 1, 2) * (1 - 2 * lax.rem(i, 2)), groups)

    def group_from(i):
        return lax.rem(
            mine + groups + groups // 2 - lax.div(i + 1, 2) * (1 - 2 * lax.rem(i, 2)), groups
        )

    def member(group, k):
        inner = lax.rem(k, per)
        a = lax.rem(lax.rem(z, span) + span - 1 - lax.div(inner, nm), span)
        return group * span + a, lax.rem(m + nm - 1 - lax.rem(inner, nm), nm)

    def member_from(group, k):
        inner = lax.rem(k, per)
        a = lax.rem(lax.rem(z, span) + 1 + lax.div(inner, nm), span)
        return group * span + a, lax.rem(m + 1 + lax.rem(inner, nm), nm)

    def ahead(k):
        return member(group_of(lax.div(k, per)), k)

    def behind(k):
        return member_from(group_from(lax.div(k, per)), k)

    def out_copy(k):
        pz, pm = ahead(k)
        return pltpu.make_async_remote_copy(
            src_ref=values_ref.at[pz * nm + pm],
            dst_ref=arrived.at[me],
            send_sem=send_out.at[k],
            recv_sem=recv_out.at[k],
            device_id={"zon": pz, "mer": pm},
            device_id_type=pl.DeviceIdType.MESH,
        )

    def back_copy(k):
        pz, pm = behind(k)
        return pltpu.make_async_remote_copy(
            src_ref=drag.at[k],
            dst_ref=returned_ref.at[me],
            send_sem=send_back.at[k],
            recv_sem=recv_back.at[k],
            device_id={"zon": pz, "mer": pm},
            device_id_type=pl.DeviceIdType.MESH,
        )

    barrier = pltpu.get_barrier_semaphore()

    def greet(k, carry):
        pz, pm = ahead(k)
        pl.semaphore_signal(
            barrier,
            inc=1,
            device_id={"zon": pz, "mer": pm},
            device_id_type=pl.DeviceIdType.MESH,
        )
        return carry

    copies = [
        pltpu.make_async_copy(source, target, loads.at[i])
        for i, (source, target) in enumerate(
            [
                (current_hbm, current_ref),
                (blocks_hbm.at[0], blocks_ref),
                (cols_hbm.at[0], cols_ref),
                (mass_hbm.at[0], mass_ref),
                (coriolis_hbm.at[0], coriolis_ref),
                (start_hbm.at[:, 0], start_ref),
                (wind_hbm.at[:, 0], wind_ref),
                (weights_hbm, weights_ref),
                (sea_hbm, sea_ref),
                (forcing_hbm, forcing_ref),
                (excess_hbm, excess_ref),
                (mask_hbm, mask_ref),
            ]
        )
    ]
    for copy in copies:
        copy.start()
    lax.fori_loop(0, count - 1, greet, 0)

    copies[0].wait()
    for j in range(tiles):
        for c in range(2):
            for k, part in enumerate(split3(current_ref[c, :, j * LANES : (j + 1) * LANES])):
                parts[k, j * rows : (j + 1) * rows, c * LANES : (c + 1) * LANES] = part
    copies[1].wait()
    square[:devices, :pairs] = block_rows(blocks_ref[...], tiles, rows)
    turned_ids = jnp.transpose(square[...])[:pairs]
    copies[2].wait()

    def pick(i, carry):
        group = group_of(i)
        pick_group(group * per, per, turned_ids, parts, cols_ref, values_ref, lanes_ref, group)
        return carry

    lax.fori_loop(0, groups, pick, 0)
    pl.semaphore_wait(barrier, count - 1)

    def launch(k, carry):
        out_copy(k).start()
        return carry

    lax.fori_loop(0, count - 1, launch, 0)

    for copy in copies[3:]:
        copy.wait()
    prepare_kernel(sea_ref, forcing_ref, weights_ref, excess_ref, mask_ref, body_ref, edge)

    def ice(at, from_ref):
        current = (from_ref[at, 0], from_ref[at, 1])
        east, north = ice_block(
            mass_ref[at],
            coriolis_ref[at],
            (start_ref[0, at], start_ref[1, at]),
            (wind_ref[0, at], wind_ref[1, at]),
            current,
        )
        velocity_ref[0, at] = east
        velocity_ref[1, at] = north
        return drag_coeff * (east - current[0]), drag_coeff * (north - current[1])

    def invert(k):
        for r in range(0, pairs, 8):
            inverse_ref[k, r : r + 8] = inverse_rows(cols_ref[k, r : r + 8])

    own_east, own_north = ice(me, values_ref)
    invert(count - 1)
    returned_ref[me, 0] = own_east
    returned_ref[me, 1] = own_north

    rim = around(
        sizes, body_ref, edge, east_ref, west_ref, south_ref, north_ref, send_rim, recv_rim
    )
    for copy in rim:
        copy.start()

    def step(k, carry):
        out_copy(k).wait_recv()
        pz, pm = behind(k)
        east, north = ice(pz * nm + pm, arrived)
        drag[k, 0] = east
        drag[k, 1] = north
        invert(k)

        @pl.when(k > 0)
        def _():
            back_copy(k - 1).start()

        return carry

    lax.fori_loop(0, count - 1, step, 0)
    back_copy(count - 2).start()

    for copy in rim:
        copy.wait()
    tall, wide = rows + 2 * ROW_RIM, width + LANES
    half = tall // 2
    wide_tiles = wide // LANES
    known = known_rows(sizes, rows, tall)
    has_south, has_north = m < nm - 1, m > 0
    for k in range(body_ref.shape[0]):
        for t in range(tiles):
            part = slice(t * LANES, (t + 1) * LANES)
            field[t, :rows] = body_ref[k, :, part]
            field[t, rows : rows + ROW_RIM] = jnp.where(has_south, south_ref[k, :, part], 0.0)
            field[t, rows + ROW_RIM :] = jnp.where(has_north, north_ref[k, :, part], 0.0)
        field[tiles] = side_tile(k, east_ref, west_ref, known)
        for t in range(wide_tiles):
            part = slice(t * LANES, (t + 1) * LANES)
            halves_ref[k, 0, :, part] = field[t, pl.ds(0, half, stride=2), :]
            halves_ref[k, 1, :, part] = field[t, pl.ds(1, half, stride=2), :]

    def collect(i, carry):
        group = group_of(i)

        def arrive(k, inner):
            back_copy(k).wait_recv()
            return inner

        lax.fori_loop(i * per, jnp.minimum(i * per + per, count - 1), arrive, 0)
        added = put_group(
            group * per, per, returned_ref, inverse_ref, lanes_ref, group, rows * tiles
        )

        @pl.when(i == 0)
        def _():
            total[...] = added

        @pl.when(i > 0)
        def _():
            total[...] += added

        return carry

    lax.fori_loop(0, groups, collect, 0)
    for c in range(2):
        for j in range(tiles):
            stress_ref[c, :, j * LANES : (j + 1) * LANES] = total[
                j * rows : (j + 1) * rows, c * LANES : (c + 1) * LANES
            ]
    pack_edges([stress_ref.at[0], stress_ref.at[1]], stress_edge)
    late = around(
        sizes, stress_ref, stress_edge, late_east, late_west, late_south, late_north,
        send_late, recv_late,
    )
    for copy in late:
        copy.start()

    def finish(k, carry):
        out_copy(k).wait_send()
        back_copy(k).wait_send()
        return carry

    lax.fori_loop(0, count - 1, finish, 0)
    for copy in late:
        copy.wait()


def pack_edges(refs, edge_ref):
    rows, width = refs[0].shape
    per = LANES // COL_RIM
    slot = lax.broadcasted_iota(jnp.int32, (rows, LANES), 1) // COL_RIM
    for start in range(0, len(refs), per):
        tile = start // per
        first = jnp.zeros((rows, LANES), jnp.float32)
        last = first
        for k, ref in enumerate(refs[start : start + per]):
            head = ref[:, :LANES]
            tail = ref[:, width - LANES :]
            if k:
                head = pltpu.roll(head, k * COL_RIM, 1)
            if (k + 1) * COL_RIM != LANES:
                tail = pltpu.roll(tail, (k + 1) * COL_RIM, 1)
            first = jnp.where(slot == k, head, first)
            last = jnp.where(slot == k, tail, last)
        edge_ref[0, :, tile * LANES : (tile + 1) * LANES] = first
        edge_ref[1, :, tile * LANES : (tile + 1) * LANES] = last


def prepare_kernel(sea_ref, forcing_ref, weights_ref, excess_ref, mask_ref, out_ref, edge_ref):
    total = weights_ref[0]
    for k in range(1, 8):
        total = total + weights_ref[k]
    ocean = mask_ref[...] > 0
    inverse = jnp.where(ocean, 1.0 / ((1.0 + excess_ref[...]) * total), 0.0)
    for k in range(8):
        out_ref[k] = weights_ref[k] * inverse
    out_ref[8] = inverse
    out_ref[9] = jnp.where(ocean, sea_ref[...], 0.0)
    out_ref[10] = forcing_ref[...]
    pack_edges([out_ref.at[k] for k in range(out_ref.shape[0])], edge_ref)


def sweep_kernel(
    sizes,
    halves_ref, stress_ref, late_east, late_west, late_south, late_north, velocity_ref,
    out_ref, velocity_hbm,
    wide_ref, tile_ref, even_ref, odd_ref, write,
):
    _, rows, width = stress_ref.shape
    tall, wide = rows + 2 * ROW_RIM, width + LANES
    half = tall // 2
    tiles = wide // LANES
    write_velocity = pltpu.make_async_copy(velocity_ref, velocity_hbm, write)
    write_velocity.start()
    m = lax.axis_index("mer")
    has_south, has_north = m < sizes[1] - 1, m > 0
    known = known_rows(sizes, rows, tall)
    for c in range(2):
        wide_ref[c, :rows, :width] = stress_ref[c]
        wide_ref[c, rows : rows + ROW_RIM, :width] = jnp.where(has_south, late_south[c], 0.0)
        wide_ref[c, rows + ROW_RIM :, :width] = jnp.where(has_north, late_north[c], 0.0)
        wide_ref[c, :, width:] = side_tile(c, late_east, late_west, known)
    east_stress = wide_ref[0]
    north_stress = wide_ref[1]
    change = (
        pltpu.roll(north_stress, wide - 1, 1)
        - pltpu.roll(north_stress, 1, 1)
        - pltpu.roll(east_stress, tall - 1, 0)
        + pltpu.roll(east_stress, 1, 0)
    )
    for t in range(tiles):
        tile_ref[t] = change[:, t * LANES : (t + 1) * LANES]

    def take(k, which):
        return halves_ref[k, which]

    for which in range(2):
        rows_of = pl.ds(which, half, stride=2)
        for t in range(tiles):
            part = slice(t * LANES, (t + 1) * LANES)
            wide_ref[which, :half, part] = (
                halves_ref[10, which, :, part] + tile_ref[t, rows_of, :]
            ) * halves_ref[8, which, :, part]

    column_odd = lax.broadcasted_iota(jnp.int32, (half, wide), 1) % 2
    even_ref[...] = take(9, 0)
    odd_ref[...] = take(9, 1)

    def phase(own_ref, other_ref, odd, colours):
        base = wide_ref[odd, :half]
        other = other_ref[...]
        if odd:
            above, below = other, pltpu.roll(other, half - 1, 0)
        else:
            above, below = pltpu.roll(other, 1, 0), other
        base = base + take(2, odd) * below + take(3, odd) * above
        base = base + take(4, odd) * pltpu.roll(below, wide - 1, 1)
        base = base + take(5, odd) * pltpu.roll(below, 1, 1)
        base = base + take(6, odd) * pltpu.roll(above, wide - 1, 1)
        base = base + take(7, odd) * pltpu.roll(above, 1, 1)
        own = own_ref[...]
        for parity in colours:
            new = base + take(0, odd) * pltpu.roll(own, wide - 1, 1)
            new = new + take(1, odd) * pltpu.roll(own, 1, 1)
            own = jnp.where(column_odd == parity, new, own)
        own_ref[...] = own

    runs = [(0, [0, 1])]
    for _ in range(SWEEPS):
        runs += [(1, [0, 1, 0]), (0, [1, 0, 1])]
    runs[-1] = (0, [1, 0])
    for odd, colours in runs:
        if odd:
            phase(odd_ref, even_ref, 1, colours)
        else:
            phase(even_ref, odd_ref, 0, colours)
    for t in range(tiles - 1):
        part = slice(t * LANES, (t + 1) * LANES)
        tile_ref[t, pl.ds(0, rows // 2, stride=2), :] = even_ref[: rows // 2, part]
        tile_ref[t, pl.ds(1, rows // 2, stride=2), :] = odd_ref[: rows // 2, part]
        out_ref[:, part] = tile_ref[t, :rows, :]
    write_velocity.wait()


def local(
    sea_level,
    forcing,
    link_weights,
    excess,
    ocean_mask,
    current,
    intersection_block,
    intersection_cols,
    ice_mass,
    coriolis,
    ice_start,
    wind_stress,
):
    rows, width = sea_level.shape
    _, devices, pairs, block = intersection_cols.shape
    slots = devices * pairs
    tiles = width // LANES
    f32 = jnp.float32
    ice_shape = (devices, pairs, block)
    slot_bytes = slots * block * 4
    sizes = (lax.axis_size("zon"), lax.axis_size("mer"))
    arrays = 11
    tall, wide = rows + 2 * ROW_RIM, width + LANES
    edge_width = -(-arrays * COL_RIM // LANES) * LANES
    dma = pltpu.SemaphoreType.DMA
    shape = jax.ShapeDtypeStruct
    stay = functools.partial(pltpu.with_memory_space_constraint, memory_space=pltpu.HBM)
    velocity, halves, *late = pl.pallas_call(
        functools.partial(travel_kernel, sizes),
        out_shape=(
            shape((2,) + ice_shape, f32),
            shape((arrays, 2, tall // 2, wide), f32),
            shape((2, rows, width), f32),
            shape((tall, LANES), f32),
            shape((tall, LANES), f32),
            shape((2, ROW_RIM, width), f32),
            shape((2, ROW_RIM, width), f32),
        ),
        in_specs=[HBM] * 12,
        out_specs=(VM,) * 7,
        scratch_shapes=[
            pltpu.VMEM((2, rows, width), f32),
            pltpu.VMEM((devices, pairs), jnp.int32),
            pltpu.VMEM((LANES, LANES), jnp.int32),
            pltpu.VMEM(ice_shape, jnp.int32),
            pltpu.VMEM(ice_shape, f32),
            pltpu.VMEM(ice_shape, f32),
            pltpu.VMEM((2,) + ice_shape, f32),
            pltpu.VMEM((2,) + ice_shape, f32),
            pltpu.VMEM((rows, width), f32),
            pltpu.VMEM((rows, width), f32),
            pltpu.VMEM((8, rows, width), f32),
            pltpu.VMEM((rows, width), f32),
            pltpu.VMEM((rows, width), jnp.int32),
            pltpu.VMEM((3, rows * tiles, 2 * LANES), jnp.bfloat16),
            pltpu.VMEM((slots // LANES, 8, LANES), jnp.int32),
            pltpu.VMEM((devices, 2, pairs, block), f32),
            pltpu.VMEM((devices, 2, pairs, block), f32),
            pltpu.VMEM((devices, 2, pairs, block), f32),
            pltpu.VMEM((devices, 2, pairs, block), f32),
            pltpu.VMEM(ice_shape, jnp.int32),
            pltpu.VMEM((rows * tiles, 2 * LANES), f32),
            pltpu.VMEM((arrays, rows, width), f32),
            pltpu.VMEM((2, rows, edge_width), f32),
            pltpu.VMEM((tall, edge_width), f32),
            pltpu.VMEM((tall, edge_width), f32),
            pltpu.VMEM((arrays, ROW_RIM, width), f32),
            pltpu.VMEM((arrays, ROW_RIM, width), f32),
            pltpu.VMEM((wide // LANES, tall, LANES), f32),
            pltpu.VMEM((2, rows, LANES), f32),
            dma((12,)),
            dma((devices,)),
            dma((devices,)),
            dma((devices,)),
            dma((devices,)),
            dma((8,)),
            dma((8,)),
            dma((8,)),
            dma((8,)),
        ],
        compiler_params=pltpu.CompilerParams(
            vmem_limit_bytes=TRAVEL_VMEM, collective_id=0, has_side_effects=True
        ),
        cost_estimate=cost(slots * block * 4096, 16 * slot_bytes),
        name="travel",
    )(
        stay(current),
        stay(intersection_block),
        stay(intersection_cols),
        stay(ice_mass),
        stay(coriolis),
        stay(ice_start),
        stay(wind_stress),
        stay(sea_level),
        stay(forcing),
        stay(link_weights),
        stay(excess),
        stay(ocean_mask),
    )
    surface, velocity = pl.pallas_call(
        functools.partial(sweep_kernel, sizes),
        out_shape=(shape((rows, width), f32), shape((2,) + ice_shape, f32)),
        in_specs=[VM] * 7,
        out_specs=(VM, HBM),
        scratch_shapes=[
            pltpu.VMEM((2, tall, wide), f32),
            pltpu.VMEM((wide // LANES, tall, LANES), f32),
            pltpu.VMEM((tall // 2, wide), f32),
            pltpu.VMEM((tall // 2, wide), f32),
            dma,
        ],
        compiler_params=pltpu.CompilerParams(vmem_limit_bytes=SWEEP_VMEM),
        cost_estimate=cost(rows * width * 200, rows * width * 64),
        name="sweep",
    )(halves, *late, velocity)
    return (surface, velocity.reshape((2, 1) + ice_shape))


def solution(mesh):
    return jax.shard_map(
        local,
        mesh=mesh,
        in_specs=(
            P("mer", "zon"),
            P("mer", "zon"),
            P(None, "mer", "zon"),
            P("mer", "zon"),
            P("mer", "zon"),
            P(None, "mer", "zon"),
            P(("zon", "mer"), None, None),
            P(("zon", "mer"), None, None, None),
            P(("zon", "mer"), None, None, None),
            P(("zon", "mer"), None, None, None),
            P(None, ("zon", "mer"), None, None, None),
            P(None, ("zon", "mer"), None, None, None),
        ),
        out_specs=(P("mer", "zon"), P(None, ("zon", "mer"), None, None, None)),
        check_vma=False,
    )
```

profile of v0, /device:TPU:0, one launch (start us, length us, event | category | flops | bytes accessed | tf_op | source)
XLA Modules:
  0.0 69.4 jit_solution(18286222214294493976)
XLA Ops:
  0.6 64.5 %travel.1 = (f32[2,32,32,128]{3,2,1,0:T(8,128)S(1)}, f32[11,2,72,640]{3,2,1,0:T(8,128)S(1)}, f32[2,128,512]{2,1,0:T(8,128)S(1)}, f32[144,128]{1,0:T(8,128)S(1)},...) custom-call(f32[2,128,512]{2,1,0:T(8,128)} %current_hbm.1, s32[1,32,32]{2,1,0:T(8,128)} %blocks_hbm.1, ...), custom_call_target="tpu_custom_call" | custom-call | flops 536870912 | bytes 8388608 | tf_op jit(solution)/shard_map/travel/pallas_call | solution.py:582
  65.2 4.2 %sweep.1 = (f32[128,512]{1,0:T(8,128)}, f32[2,32,32,128]{3,2,1,0:T(8,128)}) custom-call(f32[11,2,72,640]{3,2,1,0:T(8,128)S(1)} %get-tuple-element.11.halves_ref, f32[2,128,512]{2,1,0:T(8,128)S(1)} %get-tuple-element.12.stress_ref, f32[144,128]{1,0:T(8,128)S(1)} %get-tuple-element.13.late_east, f32[144,128]{1,0:T(8,128)S(1)} %get-tuple-element.14.late_west, ...), custom_call_target="tpu_custom_call" | custom-call | flops 13107200 | bytes 4194304 | tf_op jit(solution)/shard_map/sweep/pallas_call | solution.py:654
where the time goes:
time: 69.6 us; the launch traced here: 69.4 us
  Pallas kernels  68.8 us (99%)
    pallas_call x1, Pallas kernels, local(): pl.pallas_call(functools.partial(travel_kernel, sizes), out_shape=(shape(...  64.5 us
    pallas_call x1, Pallas kernels, local(): pl.pallas_call(functools.partial(sweep_kernel, sizes), out_shape=(shape((...  4.24 us

commit v1 on v0

--- a/solution.py
+++ b/solution.py
@@ -12,6 +12,10 @@
 ROW_RIM = 8
 COL_RIM = 16
 LANES = 128
+EAST_COLS = 11
+WEST_COLS = 12
+EXTRA_COLS = 8
+FIELD = 9
 
 drag_coeff = 1.0
 link_coeff = 0.5
@@ -96,8 +100,6 @@
 
 def around(sizes, body_ref, edge_ref, east_ref, west_ref, south_ref, north_ref, send, recv):
     rows = body_ref.shape[1]
-    nz, nm = sizes
-    z, m = lax.axis_index("zon"), lax.axis_index("mer")
     top, end = pl.ds(0, ROW_RIM), pl.ds(rows - ROW_RIM, ROW_RIM)
     whole, after, before = pl.ds(0, rows), pl.ds(rows, ROW_RIM), pl.ds(rows + ROW_RIM, ROW_RIM)
     moves = [
@@ -110,6 +112,12 @@
         (edge_ref.at[1, top], west_ref.at[after], 1, -1),
         (edge_ref.at[1, end], west_ref.at[before], 1, 1),
     ]
+    return neighbour_copies(sizes, moves, send, recv)
+
+
+def neighbour_copies(sizes, moves, send, recv):
+    nz, nm = sizes
+    z, m = lax.axis_index("zon"), lax.axis_index("mer")
     return [
         pltpu.make_async_remote_copy(
             src_ref=source,
@@ -190,6 +198,102 @@
     lower = jnp.where(m == sizes[1] - 1, rows, rows + ROW_RIM)
     upper = jnp.where(m == 0, tall, rows + ROW_RIM)
     return (row < lower) | ((row >= rows + ROW_RIM) & (row >= upper))
+
+
+def rim_lanes(arrays):
+    order = [k for k in range(arrays) if k != FIELD] + [FIELD]
+    return [(k, i * EAST_COLS, i * WEST_COLS) for i, k in enumerate(order)]
+
+
+def pack_rims(body_ref, edge_ref):
+    arrays, rows, width = body_ref.shape
+    lane = lax.broadcasted_iota(jnp.int32, (rows, LANES), 1)
+    first = jnp.zeros((rows, LANES), jnp.float32)
+    last = first
+    for k, east, west in rim_lanes(arrays):
+        head = body_ref[k, :, :LANES]
+        tail = body_ref[k, :, width - LANES :]
+        if east:
+            head = pltpu.roll(head, east, 1)
+        first = jnp.where(lane >= east, head, first)
+        if k == FIELD:
+            last = jnp.where(lane >= west, tail, last)
+        else:
+            tail = pltpu.roll(tail, west + WEST_COLS, 1)
+            last = jnp.where((lane >= west) & (lane < west + WEST_COLS), tail, last)
+    edge_ref[0, :rows] = first
+    edge_ref[1, :rows] = last
+    near = lane[:ROW_RIM]
+    extra = jnp.zeros((ROW_RIM, LANES), jnp.float32)
+    for g in range(rows // ROW_RIM):
+        piece = body_ref[FIELD, g * ROW_RIM : (g + 1) * ROW_RIM, width - LANES :]
+        at = g * EXTRA_COLS
+        shift = (at + COL_RIM) % LANES
+        if shift:
+            piece = pltpu.roll(piece, shift, 1)
+        extra = jnp.where((near >= at) & (near < at + EXTRA_COLS), piece, extra)
+    edge_ref[1, rows : rows + ROW_RIM] = extra
+    edge_ref[0, rows : rows + ROW_RIM] = extra
+
+
+def rim_moves(sizes, body_ref, edge_ref, east_ref, west_ref, south_ref, north_ref, send, recv):
+    rows = body_ref.shape[1]
+    end = rows - ROW_RIM
+
+    def part(at, count=ROW_RIM):
+        return pl.ds(at, count)
+
+    return neighbour_copies(
+        sizes,
+        [
+            (edge_ref.at[0, part(0, rows)], east_ref.at[part(0, rows)], -1, 0),
+            (edge_ref.at[1], west_ref.at[part(0, rows + ROW_RIM)], 1, 0),
+            (body_ref.at[:, part(0)], south_ref, 0, -1),
+            (body_ref.at[:, part(end)], north_ref, 0, 1),
+            (edge_ref.at[0, part(0)], east_ref.at[part(rows)], -1, -1),
+            (edge_ref.at[0, part(end)], east_ref.at[part(rows + ROW_RIM)], -1, 1),
+            (edge_ref.at[1, part(0)], west_ref.at[part(rows + ROW_RIM)], 1, -1),
+            (edge_ref.at[1, part(end)], west_ref.at[part(rows + 2 * ROW_RIM)], 1, 1),
+            (edge_ref.at[1, part(rows)], west_ref.at[part(rows + 3 * ROW_RIM)], 1, -1),
+            (edge_ref.at[1, part(rows)], west_ref.at[part(rows + 4 * ROW_RIM)], 1, 1),
+        ],
+        send,
+        recv,
+    )
+
+
+def extra_columns(west_ref, rows):
+    pieces = []
+    for g in range(rows // ROW_RIM):
+        shift = (2 * LANES - COL_RIM - g * EXTRA_COLS) % LANES
+        piece = west_ref[rows : rows + ROW_RIM]
+        pieces.append(pltpu.roll(piece, shift, 1) if shift else piece)
+    south = west_ref[rows + 3 * ROW_RIM : rows + 4 * ROW_RIM]
+    north = west_ref[rows + 4 * ROW_RIM : rows + 5 * ROW_RIM]
+    pieces.append(pltpu.roll(south, LANES - COL_RIM, 1))
+    last = (2 * LANES - COL_RIM - (rows // ROW_RIM - 1) * EXTRA_COLS) % LANES
+    pieces.append(pltpu.roll(north, last, 1) if last else north)
+    return jnp.concatenate(pieces, axis=0)
+
+
+def rim_tile(k, east_at, west_at, east_ref, west_ref, extra, rows, known):
+    tall = rows + 2 * ROW_RIM
+    lane = lax.broadcasted_iota(jnp.int32, (tall, LANES), 1)
+    east = east_ref[...]
+    west = jnp.concatenate(
+        [west_ref[:rows], west_ref[rows + ROW_RIM : rows + 3 * ROW_RIM]], axis=0
+    )
+    if east_at:
+        east = pltpu.roll(east, LANES - east_at, 1)
+    if k == FIELD:
+        kept, near = EAST_COLS + 1, LANES - (LANES - west_at)
+        west = jnp.where(lane >= near, west, extra)
+        first = LANES - COL_RIM
+    else:
+        kept, first = EAST_COLS, LANES - WEST_COLS
+        west = pltpu.roll(west, LANES - west_at - WEST_COLS, 1)
+    both = jnp.where(lane < kept, east, jnp.where(lane >= first, west, 0.0))
+    return jnp.where(known, both, 0.0)
 
 
 def travel_kernel(
@@ -311,14 +415,20 @@
         pick_group(group * per, per, turned_ids, parts, cols_ref, values_ref, lanes_ref, group)
         return carry
 
-    lax.fori_loop(0, groups, pick, 0)
-    pl.semaphore_wait(barrier, count - 1)
-
     def launch(k, carry):
         out_copy(k).start()
         return carry
 
-    lax.fori_loop(0, count - 1, launch, 0)
+    first = min(2, groups)
+    lax.fori_loop(0, first, pick, 0)
+    pl.semaphore_wait(barrier, count - 1)
+
+    def pick_and_launch(i, carry):
+        lax.fori_loop((i - first) * per, (i - first + 1) * per, launch, 0)
+        return pick(i, carry)
+
+    lax.fori_loop(first, groups, pick_and_launch, 0)
+    lax.fori_loop((groups - first) * per, count - 1, launch, 0)
 
     for copy in copies[3:]:
         copy.wait()
@@ -346,7 +456,7 @@
     returned_ref[me, 0] = own_east
     returned_ref[me, 1] = own_north
 
-    rim = around(
+    rim = rim_moves(
         sizes, body_ref, edge, east_ref, west_ref, south_ref, north_ref, send_rim, recv_rim
     )
     for copy in rim:
@@ -376,13 +486,14 @@
     wide_tiles = wide // LANES
     known = known_rows(sizes, rows, tall)
     has_south, has_north = m < nm - 1, m > 0
-    for k in range(body_ref.shape[0]):
+    extra = extra_columns(west_ref, rows)
+    for k, east_at, west_at in rim_lanes(body_ref.shape[0]):
         for t in range(tiles):
             part = slice(t * LANES, (t + 1) * LANES)
             field[t, :rows] = body_ref[k, :, part]
             field[t, rows : rows + ROW_RIM] = jnp.where(has_south, south_ref[k, :, part], 0.0)
             field[t, rows + ROW_RIM :] = jnp.where(has_north, north_ref[k, :, part], 0.0)
-        field[tiles] = side_tile(k, east_ref, west_ref, known)
+        field[tiles] = rim_tile(k, east_at, west_at, east_ref, west_ref, extra, rows, known)
         for t in range(wide_tiles):
             part = slice(t * LANES, (t + 1) * LANES)
             halves_ref[k, 0, :, part] = field[t, pl.ds(0, half, stride=2), :]
@@ -466,7 +577,7 @@
     out_ref[8] = inverse
     out_ref[9] = jnp.where(ocean, sea_ref[...], 0.0)
     out_ref[10] = forcing_ref[...]
-    pack_edges([out_ref.at[k] for k in range(out_ref.shape[0])], edge_ref)
+    pack_rims(out_ref, edge_ref)
 
 
 def sweep_kernel(
@@ -575,7 +686,6 @@
     sizes = (lax.axis_size("zon"), lax.axis_size("mer"))
     arrays = 11
     tall, wide = rows + 2 * ROW_RIM, width + LANES
-    edge_width = -(-arrays * COL_RIM // LANES) * LANES
     dma = pltpu.SemaphoreType.DMA
     shape = jax.ShapeDtypeStruct
     stay = functools.partial(pltpu.with_memory_space_constraint, memory_space=pltpu.HBM)
@@ -615,9 +725,9 @@
             pltpu.VMEM(ice_shape, jnp.int32),
             pltpu.VMEM((rows * tiles, 2 * LANES), f32),
             pltpu.VMEM((arrays, rows, width), f32),
-            pltpu.VMEM((2, rows, edge_width), f32),
-            pltpu.VMEM((tall, edge_width), f32),
-            pltpu.VMEM((tall, edge_width), f32),
+            pltpu.VMEM((2, rows + ROW_RIM, LANES), f32),
+            pltpu.VMEM((tall, LANES), f32),
+            pltpu.VMEM((rows + 5 * ROW_RIM, LANES), f32),
             pltpu.VMEM((arrays, ROW_RIM, width), f32),
             pltpu.VMEM((arrays, ROW_RIM, width), f32),
             pltpu.VMEM((wide // LANES, tall, LANES), f32),
@@ -627,8 +737,8 @@
             dma((devices,)),
             dma((devices,)),
             dma((devices,)),
-            dma((8,)),
-            dma((8,)),
+            dma((10,)),
+            dma((10,)),
             dma((8,)),
             dma((8,)),
         ],

time: 69.6 us -> 66.5 us (0.955)
  Pallas kernels: 68.8 us -> 65.7 us
    pallas_call x1, Pallas kernels: 64.5 us -> 61.4 us  [local(): pl.pallas_call(functools.partial(travel_kernel, sizes), out_shape=(shape(...]
where the time goes in v1:
time: 66.5 us; the launch traced here: 66.3 us
  Pallas kernels  65.7 us (99%)
    pallas_call x1, Pallas kernels, local(): pl.pallas_call(functools.partial(travel_kernel, sizes), out_shape=(shape(...  61.4 us
    pallas_call x1, Pallas kernels, local(): pl.pallas_call(functools.partial(sweep_kernel, sizes), out_shape=(shape((...  4.24 us

profile of v1, /device:TPU:0, one launch (start us, length us, event | category | flops | bytes accessed | tf_op | source)
XLA Modules:
  0.0 66.3 jit_solution(6968455503128909394)
XLA Ops:
  0.6 61.4 %travel.1 = (f32[2,32,32,128]{3,2,1,0:T(8,128)S(1)}, f32[11,2,72,640]{3,2,1,0:T(8,128)S(1)}, f32[2,128,512]{2,1,0:T(8,128)S(1)}, f32[144,128]{1,0:T(8,128)S(1)},...) custom-call(f32[2,128,512]{2,1,0:T(8,128)} %current_hbm.1, s32[1,32,32]{2,1,0:T(8,128)} %blocks_hbm.1, ...), custom_call_target="tpu_custom_call" | custom-call | flops 536870912 | bytes 8388608 | tf_op jit(solution)/shard_map/travel/pallas_call | solution.py:692
  62.1 4.2 %sweep.1 = (f32[128,512]{1,0:T(8,128)}, f32[2,32,32,128]{3,2,1,0:T(8,128)}) custom-call(f32[11,2,72,640]{3,2,1,0:T(8,128)S(1)} %get-tuple-element.11.halves_ref, f32[2,128,512]{2,1,0:T(8,128)S(1)} %get-tuple-element.12.stress_ref, f32[144,128]{1,0:T(8,128)S(1)} %get-tuple-element.13.late_east, f32[144,128]{1,0:T(8,128)S(1)} %get-tuple-element.14.late_west, ...), custom_call_target="tpu_custom_call" | custom-call | flops 13107200 | bytes 4194304 | tf_op jit(solution)/shard_map/sweep/pallas_call | solution.py:764

commit v2 on v1

--- a/solution.py
+++ b/solution.py
@@ -198,6 +198,29 @@
     lower = jnp.where(m == sizes[1] - 1, rows, rows + ROW_RIM)
     upper = jnp.where(m == 0, tall, rows + ROW_RIM)
     return (row < lower) | ((row >= rows + ROW_RIM) & (row >= upper))
+
+
+def split_columns(tiles):
+    rows = tiles[0].shape[0]
+    lane = lax.broadcasted_iota(jnp.int32, (rows, LANES), 1)
+    half = LANES // 2
+    index = 2 * (lane % half) + lane // half
+    low = lane < half
+    here = [lane_take(tile, index) for tile in tiles]
+    away = [pltpu.roll(tile, half, 1) for tile in here]
+    even, odd = [], []
+    for t in range(0, len(tiles), 2):
+        u = min(t + 1, len(tiles) - 1)
+        even.append(jnp.where(low, here[t], away[u]))
+        odd.append(jnp.where(low, away[t], here[u]))
+    return even, odd
+
+
+def join_columns(even, odd, tile):
+    rows = even.shape[0]
+    lane = lax.broadcasted_iota(jnp.int32, (rows, LANES), 1)
+    index = (tile % 2) * (LANES // 2) + lane // 2
+    return jnp.where(lane % 2 == 0, lane_take(even, index), lane_take(odd, index))
 
 
 def rim_lanes(arrays):
@@ -494,10 +517,16 @@
             field[t, rows : rows + ROW_RIM] = jnp.where(has_south, south_ref[k, :, part], 0.0)
             field[t, rows + ROW_RIM :] = jnp.where(has_north, north_ref[k, :, part], 0.0)
         field[tiles] = rim_tile(k, east_at, west_at, east_ref, west_ref, extra, rows, known)
-        for t in range(wide_tiles):
-            part = slice(t * LANES, (t + 1) * LANES)
-            halves_ref[k, 0, :, part] = field[t, pl.ds(0, half, stride=2), :]
-            halves_ref[k, 1, :, part] = field[t, pl.ds(1, half, stride=2), :]
+        for which in range(2):
+            rows_of = pl.ds(which, half, stride=2)
+            split = split_columns([field[t, rows_of, :] for t in range(wide_tiles)])
+            for odd, found in enumerate(split):
+                whole = jnp.concatenate(found, axis=1)
+                if k in (4, 6) and odd:
+                    whole = pltpu.roll(whole, 1, 1)
+                if k in (5, 7) and not odd:
+                    whole = pltpu.roll(whole, whole.shape[1] - 1, 1)
+                halves_ref[k, which, odd] = whole
 
     def collect(i, carry):
         group = group_of(i)
@@ -584,7 +613,7 @@
     sizes,
     halves_ref, stress_ref, late_east, late_west, late_south, late_north, velocity_ref,
     out_ref, velocity_hbm,
-    wide_ref, tile_ref, even_ref, odd_ref, write,
+    wide_ref, tile_ref, source_ref, field_ref, write,
 ):
     _, rows, width = stress_ref.shape
     tall, wide = rows + 2 * ROW_RIM, width + LANES
@@ -611,54 +640,57 @@
     for t in range(tiles):
         tile_ref[t] = change[:, t * LANES : (t + 1) * LANES]
 
-    def take(k, which):
-        return halves_ref[k, which]
-
+    thin = field_ref.shape[3]
     for which in range(2):
         rows_of = pl.ds(which, half, stride=2)
-        for t in range(tiles):
-            part = slice(t * LANES, (t + 1) * LANES)
-            wide_ref[which, :half, part] = (
-                halves_ref[10, which, :, part] + tile_ref[t, rows_of, :]
-            ) * halves_ref[8, which, :, part]
-
-    column_odd = lax.broadcasted_iota(jnp.int32, (half, wide), 1) % 2
-    even_ref[...] = take(9, 0)
-    odd_ref[...] = take(9, 1)
-
-    def phase(own_ref, other_ref, odd, colours):
-        base = wide_ref[odd, :half]
-        other = other_ref[...]
-        if odd:
-            above, below = other, pltpu.roll(other, half - 1, 0)
+        split = split_columns([tile_ref[t, rows_of, :] for t in range(tiles)])
+        for odd, found in enumerate(split):
+            source_ref[which, odd] = (
+                halves_ref[10, which, odd] + jnp.concatenate(found, axis=1)
+            ) * halves_ref[8, which, odd]
+            field_ref[which, odd] = halves_ref[FIELD, which, odd]
+
+    def phase(which, colours):
+        other = [field_ref[1 - which, odd] for odd in range(2)]
+        if which:
+            above = other
+            below = [pltpu.roll(value, half - 1, 0) for value in other]
         else:
-            above, below = pltpu.roll(other, 1, 0), other
-        base = base + take(2, odd) * below + take(3, odd) * above
-        base = base + take(4, odd) * pltpu.roll(below, wide - 1, 1)
-        base = base + take(5, odd) * pltpu.roll(below, 1, 1)
-        base = base + take(6, odd) * pltpu.roll(above, wide - 1, 1)
-        base = base + take(7, odd) * pltpu.roll(above, 1, 1)
-        own = own_ref[...]
+            above = [pltpu.roll(value, 1, 0) for value in other]
+            below = other
+        weight = [[halves_ref[k, which, odd] for k in range(8)] for odd in range(2)]
+        w = weight[0]
+        base_even = source_ref[which, 0] + w[2] * below[0] + w[3] * above[0]
+        base_even = base_even + w[4] * below[1] + w[6] * above[1]
+        base_even = base_even + pltpu.roll(w[5] * below[1] + w[7] * above[1], 1, 1)
+        w = weight[1]
+        base_odd = source_ref[which, 1] + w[2] * below[1] + w[3] * above[1]
+        base_odd = base_odd + w[5] * below[0] + w[7] * above[0]
+        base_odd = base_odd + pltpu.roll(w[4] * below[0] + w[6] * above[0], thin - 1, 1)
+        even, odd = field_ref[which, 0], field_ref[which, 1]
         for parity in colours:
-            new = base + take(0, odd) * pltpu.roll(own, wide - 1, 1)
-            new = new + take(1, odd) * pltpu.roll(own, 1, 1)
-            own = jnp.where(column_odd == parity, new, own)
-        own_ref[...] = own
+            if parity:
+                odd = base_odd + weight[1][0] * pltpu.roll(even, thin - 1, 1)
+                odd = odd + weight[1][1] * even
+            else:
+                even = base_even + weight[0][0] * odd
+                even = even + weight[0][1] * pltpu.roll(odd, 1, 1)
+        field_ref[which, 0] = even
+        field_ref[which, 1] = odd
 
     runs = [(0, [0, 1])]
     for _ in range(SWEEPS):
         runs += [(1, [0, 1, 0]), (0, [1, 0, 1])]
     runs[-1] = (0, [1, 0])
-    for odd, colours in runs:
-        if odd:
-            phase(odd_ref, even_ref, 1, colours)
-        else:
-            phase(even_ref, odd_ref, 0, colours)
+    for which, colours in runs:
+        phase(which, colours)
     for t in range(tiles - 1):
-        part = slice(t * LANES, (t + 1) * LANES)
-        tile_ref[t, pl.ds(0, rows // 2, stride=2), :] = even_ref[: rows // 2, part]
-        tile_ref[t, pl.ds(1, rows // 2, stride=2), :] = odd_ref[: rows // 2, part]
-        out_ref[:, part] = tile_ref[t, :rows, :]
+        at = slice(t // 2 * LANES, t // 2 * LANES + LANES)
+        for which in range(2):
+            tile_ref[t, pl.ds(which, rows // 2, stride=2), :] = join_columns(
+                field_ref[which, 0, : rows // 2, at], field_ref[which, 1, : rows // 2, at], t
+            )
+        out_ref[:, t * LANES : (t + 1) * LANES] = tile_ref[t, :rows, :]
     write_velocity.wait()
 
 
@@ -686,6 +718,7 @@
     sizes = (lax.axis_size("zon"), lax.axis_size("mer"))
     arrays = 11
     tall, wide = rows + 2 * ROW_RIM, width + LANES
+    thin = -(-wide // (2 * LANES)) * LANES
     dma = pltpu.SemaphoreType.DMA
     shape = jax.ShapeDtypeStruct
     stay = functools.partial(pltpu.with_memory_space_constraint, memory_space=pltpu.HBM)
@@ -693,7 +726,7 @@
         functools.partial(travel_kernel, sizes),
         out_shape=(
             shape((2,) + ice_shape, f32),
-            shape((arrays, 2, tall // 2, wide), f32),
+            shape((arrays, 2, 2, tall // 2, thin), f32),
             shape((2, rows, width), f32),
             shape((tall, LANES), f32),
             shape((tall, LANES), f32),
@@ -769,8 +802,8 @@
         scratch_shapes=[
             pltpu.VMEM((2, tall, wide), f32),
             pltpu.VMEM((wide // LANES, tall, LANES), f32),
-            pltpu.VMEM((tall // 2, wide), f32),
-            pltpu.VMEM((tall // 2, wide), f32),
+            pltpu.VMEM((2, 2, tall // 2, thin), f32),
+            pltpu.VMEM((2, 2, tall // 2, thin), f32),
             dma,
         ],
         compiler_params=pltpu.CompilerParams(vmem_limit_bytes=SWEEP_VMEM),

time: 66.5 us -> 65.2 us (0.980)
  Pallas kernels: 65.7 us -> 64.4 us
    pallas_call x1, Pallas kernels: 4.24 us -> 3.02 us  [local(): pl.pallas_call(functools.partial(sweep_kernel, sizes), out_shape=(shape((...]
where the time goes in v2:
time: 65.2 us; the launch traced here: 65.1 us
  Pallas kernels  64.4 us (99%)
    pallas_call x1, Pallas kernels, local(): pl.pallas_call(functools.partial(travel_kernel, sizes), out_shape=(shape(...  61.4 us
    pallas_call x1, Pallas kernels, local(): pl.pallas_call(functools.partial(sweep_kernel, sizes), out_shape=(shape((...  3.02 us

profile of v2, /device:TPU:0, one launch (start us, length us, event | category | flops | bytes accessed | tf_op | source)
XLA Modules:
  0.0 65.1 jit_solution(18436684805177513435)
XLA Ops:
  0.6 61.4 %travel.1 = (f32[2,32,32,128]{3,2,1,0:T(8,128)S(1)}, f32[11,2,2,72,384]{4,3,2,1,0:T(8,128)S(1)}, f32[2,128,512]{2,1,0:T(8,128)S(1)}, f32[144,128]{1,0:T(8,128)S(...) custom-call(f32[2,128,512]{2,1,0:T(8,128)} %current_hbm.1, ...), custom_call_target="tpu_custom_call" | custom-call | flops 536870912 | bytes 8388608 | tf_op jit(solution)/shard_map/travel/pallas_call | solution.py:725
  62.1 3.0 %sweep.1 = (f32[128,512]{1,0:T(8,128)}, f32[2,32,32,128]{3,2,1,0:T(8,128)}) custom-call(f32[11,2,2,72,384]{4,3,2,1,0:T(8,128)S(1)} %get-tuple-element.11.halves_ref, f32[2,128,512]{2,1,0:T(8,128)S(1)} %get-tuple-element.12.stress_ref, f32[144,128]{1,0:T(8,128)S(1)} %get-tuple-element.13.late_east, f32[144,128]{1,0:T(8,128)S(1)} %get-tuple-element.14.late_west, ...), custom_call_target="tpu_custom_call" | custom-call | flops 13107200 | bytes 4194304 | tf_op jit(solution)/shard_map/sweep/pallas_call | solution.py:797

commit v3 on v2

--- a/solution.py
+++ b/solution.py
@@ -98,23 +98,6 @@
     return east, north
 
 
-def around(sizes, body_ref, edge_ref, east_ref, west_ref, south_ref, north_ref, send, recv):
-    rows = body_ref.shape[1]
-    top, end = pl.ds(0, ROW_RIM), pl.ds(rows - ROW_RIM, ROW_RIM)
-    whole, after, before = pl.ds(0, rows), pl.ds(rows, ROW_RIM), pl.ds(rows + ROW_RIM, ROW_RIM)
-    moves = [
-        (edge_ref.at[0], east_ref.at[whole], -1, 0),
-        (edge_ref.at[1], west_ref.at[whole], 1, 0),
-        (body_ref.at[:, top], south_ref, 0, -1),
-        (body_ref.at[:, end], north_ref, 0, 1),
-        (edge_ref.at[0, top], east_ref.at[after], -1, -1),
-        (edge_ref.at[0, end], east_ref.at[before], -1, 1),
-        (edge_ref.at[1, top], west_ref.at[after], 1, -1),
-        (edge_ref.at[1, end], west_ref.at[before], 1, 1),
-    ]
-    return neighbour_copies(sizes, moves, send, recv)
-
-
 def neighbour_copies(sizes, moves, send, recv):
     nz, nm = sizes
     z, m = lax.axis_index("zon"), lax.axis_index("mer")
@@ -159,35 +142,84 @@
             values_ref[base + d, c] = taken[d * pairs : (d + 1) * pairs]
 
 
-def put_group(base, per, returned_ref, inverse_ref, lanes_ref, group, count):
+def put_group(base, per, returned_ref, inverse_ref, put_ref, group):
     pairs = inverse_ref.shape[1]
-    row = lax.broadcasted_iota(jnp.int32, (count, LANES), 0)
-    ids = lanes_ref[group]
-    put = jnp.where(
-        jnp.broadcast_to(ids[:1], (count, LANES)) == row, 1.0, 0.0
-    ).astype(jnp.bfloat16)
+    put = put_ref[group]
     inverse = inverse_ref[pl.ds(base, per)].reshape(LANES, LANES)
     index = jnp.maximum(inverse, 0)
     halves = []
     for c in range(2):
         values = jnp.concatenate([returned_ref[base + d, c] for d in range(per)], axis=0)
         halves.append(jnp.where(inverse >= 0, lane_take(values, index), 0.0))
-    high, middle, low = split3(jnp.concatenate(halves, axis=1))
-    return nn_dot(put, high) + nn_dot(put, middle) + nn_dot(put, low)
-
-
-def side_tile(k, east_ref, west_ref, known):
-    tall = east_ref.shape[0]
+    return nn_dot(
+        jnp.concatenate([put] * 3, axis=1),
+        jnp.concatenate(split3(jnp.concatenate(halves, axis=1)), axis=0),
+    )
+
+
+def pack_late(total, edge_ref, rows):
+    parts = LANES // (2 * COL_RIM)
+    deep = rows // parts
     per = LANES // COL_RIM
-    slot = lax.broadcasted_iota(jnp.int32, (tall, LANES), 1) // COL_RIM
-    at = (k // per) * LANES
-    spot = k % per
-    east = east_ref[:, at : at + LANES]
-    west = west_ref[:, at : at + LANES]
-    if spot:
-        east = pltpu.roll(east, LANES - spot * COL_RIM, 1)
-    if spot != per - 1:
-        west = pltpu.roll(west, LANES - (spot + 1) * COL_RIM, 1)
+    slot = lax.broadcasted_iota(jnp.int32, (deep, LANES), 1) // COL_RIM
+    first = jnp.zeros((deep, LANES), jnp.float32)
+    last = first
+    for spot in range(per):
+        at = (spot // 2) * deep
+        lanes = slice(spot % 2 * LANES, (spot % 2 + 1) * LANES)
+        head = total[at : at + deep, lanes]
+        tail = total[total.shape[0] - rows + at : total.shape[0] - rows + at + deep, lanes]
+        if spot:
+            head = pltpu.roll(head, spot * COL_RIM, 1)
+        if spot != per - 1:
+            tail = pltpu.roll(tail, (spot + 1) * COL_RIM, 1)
+        first = jnp.where(slot == spot, head, first)
+        last = jnp.where(slot == spot, tail, last)
+    edge_ref[0] = first
+    edge_ref[1] = last
+
+
+def late_moves(sizes, stress_ref, edge_ref, east_ref, west_ref, south_ref, north_ref, send, recv):
+    rows, deep = stress_ref.shape[1], edge_ref.shape[1]
+
+    def part(at, count=ROW_RIM):
+        return pl.ds(at, count)
+
+    return neighbour_copies(
+        sizes,
+        [
+            (edge_ref.at[0], east_ref.at[part(0, deep)], -1, 0),
+            (edge_ref.at[1], west_ref.at[part(0, deep)], 1, 0),
+            (edge_ref.at[0, part(0)], east_ref.at[part(deep)], -1, -1),
+            (edge_ref.at[0, part(deep - ROW_RIM)], east_ref.at[part(deep + ROW_RIM)], -1, 1),
+            (edge_ref.at[1, part(0)], west_ref.at[part(deep)], 1, -1),
+            (edge_ref.at[1, part(deep - ROW_RIM)], west_ref.at[part(deep + ROW_RIM)], 1, 1),
+            (stress_ref.at[:, part(0)], south_ref, 0, -1),
+            (stress_ref.at[:, part(rows - ROW_RIM)], north_ref, 0, 1),
+        ],
+        send,
+        recv,
+    )
+
+
+def late_tile(c, east_ref, west_ref, known):
+    per = LANES // COL_RIM
+    parts = per // 2
+    deep = east_ref.shape[0] - 2 * ROW_RIM
+
+    def spread(ref, target):
+        spots = [(0, deep, 2 * q + c) for q in range(parts)]
+        spots += [(deep, ROW_RIM, c), (deep + ROW_RIM, ROW_RIM, 2 * parts - 2 + c)]
+        pieces = []
+        for at, count, spot in spots:
+            shift = (target - spot) % per * COL_RIM
+            piece = ref[at : at + count]
+            pieces.append(pltpu.roll(piece, shift, 1) if shift else piece)
+        return jnp.concatenate(pieces, axis=0)
+
+    east = spread(east_ref, 0)
+    west = spread(west_ref, per - 1)
+    slot = lax.broadcasted_iota(jnp.int32, east.shape, 1) // COL_RIM
     both = jnp.where(slot == 0, east, jnp.where(slot == per - 1, west, 0.0))
     return jnp.where(known, both, 0.0)
 
@@ -326,7 +358,7 @@
     velocity_ref, halves_ref, stress_ref, late_east, late_west, late_south, late_north,
     current_ref, blocks_ref, square, cols_ref, mass_ref, coriolis_ref, start_ref, wind_ref,
     sea_ref, forcing_ref, weights_ref, excess_ref, mask_ref,
-    parts, lanes_ref, values_ref, arrived, drag, returned_ref, inverse_ref, total,
+    parts, lanes_ref, put_ref, values_ref, arrived, drag, returned_ref, inverse_ref, total,
     body_ref, edge, east_ref, west_ref, south_ref, north_ref, field, stress_edge,
     loads, send_out, recv_out, send_back, recv_back, send_rim, recv_rim, send_late, recv_late,
 ):
@@ -528,7 +560,18 @@
                     whole = pltpu.roll(whole, whole.shape[1] - 1, 1)
                 halves_ref[k, which, odd] = whole
 
-    def collect(i, carry):
+    total[...] = jnp.zeros_like(total)
+    row = lax.broadcasted_iota(jnp.int32, (rows * tiles, LANES), 0)
+
+    def place(group, carry):
+        ids = jnp.broadcast_to(lanes_ref[group][:1], row.shape)
+        put_ref[group] = jnp.where(ids == row, 1.0, 0.0).astype(jnp.bfloat16)
+        return carry
+
+    lax.fori_loop(0, groups, place, 0)
+
+    def collect(turn, carry):
+        i = lax.rem(turn + groups - 1, groups)
         group = group_of(i)
 
         def arrive(k, inner):
@@ -537,27 +580,20 @@
 
         lax.fori_loop(i * per, jnp.minimum(i * per + per, count - 1), arrive, 0)
         added = put_group(
-            group * per, per, returned_ref, inverse_ref, lanes_ref, group, rows * tiles
+            group * per, per, returned_ref, inverse_ref, put_ref, group
         )
 
-        @pl.when(i == 0)
-        def _():
-            total[...] = added
-
-        @pl.when(i > 0)
-        def _():
-            total[...] += added
-
+        total[...] += added
         return carry
 
     lax.fori_loop(0, groups, collect, 0)
+    pack_late(total, stress_edge, rows)
     for c in range(2):
         for j in range(tiles):
             stress_ref[c, :, j * LANES : (j + 1) * LANES] = total[
                 j * rows : (j + 1) * rows, c * LANES : (c + 1) * LANES
             ]
-    pack_edges([stress_ref.at[0], stress_ref.at[1]], stress_edge)
-    late = around(
+    late = late_moves(
         sizes, stress_ref, stress_edge, late_east, late_west, late_south, late_north,
         send_late, recv_late,
     )
@@ -572,27 +608,6 @@
     lax.fori_loop(0, count - 1, finish, 0)
     for copy in late:
         copy.wait()
-
-
-def pack_edges(refs, edge_ref):
-    rows, width = refs[0].shape
-    per = LANES // COL_RIM
-    slot = lax.broadcasted_iota(jnp.int32, (rows, LANES), 1) // COL_RIM
-    for start in range(0, len(refs), per):
-        tile = start // per
-        first = jnp.zeros((rows, LANES), jnp.float32)
-        last = first
-        for k, ref in enumerate(refs[start : start + per]):
-            head = ref[:, :LANES]
-            tail = ref[:, width - LANES :]
-            if k:
-                head = pltpu.roll(head, k * COL_RIM, 1)
-            if (k + 1) * COL_RIM != LANES:
-                tail = pltpu.roll(tail, (k + 1) * COL_RIM, 1)
-            first = jnp.where(slot == k, head, first)
-            last = jnp.where(slot == k, tail, last)
-        edge_ref[0, :, tile * LANES : (tile + 1) * LANES] = first
-        edge_ref[1, :, tile * LANES : (tile + 1) * LANES] = last
 
 
 def prepare_kernel(sea_ref, forcing_ref, weights_ref, excess_ref, mask_ref, out_ref, edge_ref):
@@ -628,7 +643,7 @@
         wide_ref[c, :rows, :width] = stress_ref[c]
         wide_ref[c, rows : rows + ROW_RIM, :width] = jnp.where(has_south, late_south[c], 0.0)
         wide_ref[c, rows + ROW_RIM :, :width] = jnp.where(has_north, late_north[c], 0.0)
-        wide_ref[c, :, width:] = side_tile(c, late_east, late_west, known)
+        wide_ref[c, :, width:] = late_tile(c, late_east, late_west, known)
     east_stress = wide_ref[0]
     north_stress = wide_ref[1]
     change = (
@@ -719,6 +734,7 @@
     arrays = 11
     tall, wide = rows + 2 * ROW_RIM, width + LANES
     thin = -(-wide // (2 * LANES)) * LANES
+    deep = rows * 2 * COL_RIM // LANES
     dma = pltpu.SemaphoreType.DMA
     shape = jax.ShapeDtypeStruct
     stay = functools.partial(pltpu.with_memory_space_constraint, memory_space=pltpu.HBM)
@@ -728,8 +744,8 @@
             shape((2,) + ice_shape, f32),
             shape((arrays, 2, 2, tall // 2, thin), f32),
             shape((2, rows, width), f32),
-            shape((tall, LANES), f32),
-            shape((tall, LANES), f32),
+            shape((deep + 2 * ROW_RIM, LANES), f32),
+            shape((deep + 2 * ROW_RIM, LANES), f32),
             shape((2, ROW_RIM, width), f32),
             shape((2, ROW_RIM, width), f32),
         ),
@@ -751,6 +767,7 @@
             pltpu.VMEM((rows, width), jnp.int32),
             pltpu.VMEM((3, rows * tiles, 2 * LANES), jnp.bfloat16),
             pltpu.VMEM((slots // LANES, 8, LANES), jnp.int32),
+            pltpu.VMEM((slots // LANES, rows * tiles, LANES), jnp.bfloat16),
             pltpu.VMEM((devices, 2, pairs, block), f32),
             pltpu.VMEM((devices, 2, pairs, block), f32),
             pltpu.VMEM((devices, 2, pairs, block), f32),
@@ -764,7 +781,7 @@
             pltpu.VMEM((arrays, ROW_RIM, width), f32),
             pltpu.VMEM((arrays, ROW_RIM, width), f32),
             pltpu.VMEM((wide // LANES, tall, LANES), f32),
-            pltpu.VMEM((2, rows, LANES), f32),
+            pltpu.VMEM((2, deep, LANES), f32),
             dma((12,)),
             dma((devices,)),
             dma((devices,)),

time: 65.2 us -> 63.7 us (0.977)
  Pallas kernels: 64.4 us -> 62.7 us
    pallas_call x1, Pallas kernels: 61.4 us -> 59.6 us  [local(): pl.pallas_call(functools.partial(travel_kernel, sizes), out_shape=(shape(...]
where the time goes in v3:
time: 63.7 us; the launch traced here: 63.3 us
  Pallas kernels  62.7 us (98%)
  between operations  0.64 us (1%)
    pallas_call x1, Pallas kernels, local(): pl.pallas_call(functools.partial(travel_kernel, sizes), out_shape=(shape(...  59.6 us
    pallas_call x1, Pallas kernels, local(): pl.pallas_call(functools.partial(sweep_kernel, sizes), out_shape=(shape((...  3.05 us

profile of v3, /device:TPU:0, one launch (start us, length us, event | category | flops | bytes accessed | tf_op | source)
XLA Modules:
  0.0 63.3 jit_solution(7269604305187846533)
XLA Ops:
  0.6 59.6 %travel.1 = (f32[2,32,32,128]{3,2,1,0:T(8,128)S(1)}, f32[11,2,2,72,384]{4,3,2,1,0:T(8,128)S(1)}, f32[2,128,512]{2,1,0:T(8,128)S(1)}, f32[48,128]{1,0:T(8,128)S(1...) custom-call(f32[2,128,512]{2,1,0:T(8,128)} %current_hbm.1, s32[1,32,32]{2,1,0:T(8,128)} %blocks_hbm.1, ...), custom_call_target="tpu_custom_call" | custom-call | flops 536870912 | bytes 8388608 | tf_op jit(solution)/shard_map/travel/pallas_call | solution.py:741
  60.3 3.0 %sweep.1 = (f32[128,512]{1,0:T(8,128)}, f32[2,32,32,128]{3,2,1,0:T(8,128)}) custom-call(f32[11,2,2,72,384]{4,3,2,1,0:T(8,128)S(1)} %get-tuple-element.11.halves_ref, f32[2,128,512]{2,1,0:T(8,128)S(1)} %get-tuple-element.12.stress_ref, f32[48,128]{1,0:T(8,128)S(1)} %get-tuple-element.13.late_east, f32[48,128]{1,0:T(8,128)S(1)} %get-tuple-element.14.late_west, ...), custom_call_target="tpu_custom_call" | custom-call | flops 13107200 | bytes 4194304 | tf_op jit(solution)/shard_map/sweep/pallas_call | solution.py:814
